TPU v7x, 32 devices: a whole 2x2x4 slice. The times are simulated.
32 devices in a mesh: groups: 2 (over x), blk: 4 (over y, core), col: 4 (over z).
Axes of the slice: x: 2, y: 2, z: 4, core: 2. Of those that a mesh axis runs over, the one named last changes fastest.
Arguments:
- pair_block: bfloat16 [4096, 16384], P(('groups', 'blk'), 'col'), parts along dimension 0, may hold values from -1.5 to 1.5
- occ_energy: float32 [2], P('groups'), parts along dimension 0, may hold values from -1.5 to -0.3
- virt_energy: float32 [4096], P('groups'), parts along dimension 0, may hold values from 0.2 to 3
- frequency: float32 [2], P('groups'), parts along dimension 0, may hold values from 0.2 to 2
Outputs:
- dielectric: float32 [32768, 16384], P(('groups', 'col'), 'blk'), parts along dimension 0
There are 2 independent parts, one for each index of `groups`. A program takes and returns all parts, laid end to end along the dimension named above; each array names one. Nothing has to cross between parts.
All inputs are finite; a program needn't handle non-finite values.
Results may differ from a plain program's by a relative error of at most 0.0027.
Values may be sent and summed in bfloat16 or wider, within the bound.
No kernel may reach another device: no remote copies, remote signals or barrier semaphores. Data moves between devices by JAX's collectives and lax.ppermute only.
A program may use at most 192 MiB of HBM per device.

v0:
```python
import jax
import jax.numpy as jnp
from jax import lax
from jax.sharding import PartitionSpec as P


def pair_weights(occ_energy, virt_energy, frequency):
    gap = (virt_energy[None, :] - occ_energy[:, None]).reshape(-1)
    return 2.0 * gap / (gap * gap + frequency[0] * frequency[0])


def shards(pair_block, occ_energy, virt_energy, frequency):
    weights = pair_weights(occ_energy, virt_energy, frequency)
    row_full = lax.all_gather(pair_block, "col", axis=1, tiled=True)
    column_slab = lax.all_to_all(row_full, "blk", split_axis=1, concat_axis=0, tiled=True)
    scaled = (
        lax.all_gather(pair_block, "blk", axis=0, tiled=True).astype(jnp.float32) * weights[:, None]
    ).astype(jnp.bfloat16)
    return lax.dot_general(
        scaled, column_slab, (((0,), (0,)), ((), ())), preferred_element_type=jnp.float32
    )


def solution(mesh):
    return jax.shard_map(
        shards,
        mesh=mesh,
        in_specs=(P(("groups", "blk"), "col"), P("groups"), P("groups"), P("groups")),
        out_specs=P(("groups", "col"), "blk"),
        check_vma=False,
    )
```

profile of v0, /device:TPU:0, one launch (start us, length us, event | category | flops | bytes accessed | tf_op | source)
XLA Modules:
  0.0 691.5 jit_solution(8358652491445676149)
XLA Ops:
  6.5 0.0 all-gather.5.cloned.1.call-start
  6.5 6.4 copy.5
  12.9 0.0 all-gather.5.cloned.1.call-update
  13.0 0.0 all-gather.3.cloned.1.call-start
  13.0 0.7 all-gather.3.cloned.1.call-update
  13.7 288.9 %all-gather.5.cloned.1.call-done = bf16[512,16384]{0,1:T(8,128)(2,1)} async-done(((bf16[512,4096]{0,1:T(8,128)(2,1)}), bf16[512,16384]{0,1:T(8,128)(2,1)}) %all-gather.5.cloned.1.call-update) | async-done | bytes 16777232 | tf_op jit(solution)/shard_map/all_gather | solution.py:14
  302.6 0.0 copy-start
  302.6 7.3 %all-to-all-start = ((bf16[512,4,4096]{0,2,1:T(8,128)(2,1)}), bf16[512,4,4096]{0,2,1:T(8,128)(2,1)}, u32[]{:S(2)}, u32[]{:S(2)}) async-start(bf16[512,4,4096]{0,2,1:T(8,128)(2,1)} %bitcast.8), calls=%async_computation | async-start | bytes 33554432 | tf_op jit(solution)/shard_map/all_to_all | solution.py:15
  311.2 0.0 copy-done
  311.2 271.6 %all-to-all-done = bf16[512,4,4096]{0,2,1:T(8,128)(2,1)} async-done(((bf16[512,4,4096]{0,2,1:T(8,128)(2,1)}), bf16[512,4,4096]{0,2,1:T(8,128)(2,1)}, u32[]{:S(2)}, u32[]{:S(2)}) %all-to-all-start) | async-done | bytes 16777248 | tf_op jit(solution)/shard_map/all_to_all | solution.py:15
  582.8 20.7 %copy.6 = bf16[4,512,4096]{2,1,0:T(8,128)(2,1)} copy(bf16[4,512,4096]{1,2,0:T(8,128)(2,1)} %bitcast.3) | data formatting | bytes 33554432 | tf_op jit(solution)/shard_map/all_to_all | solution.py:15
  603.5 0.0 all-gather.3.cloned.1.call-done
  603.5 81.2 %fusion = f32[4096,4096]{1,0:T(8,128)} fusion(bf16[2048,4096]{1,0:T(8,128)(2,1)} %bitcast.9, bf16[2048,4096]{1,0:T(8,128)(2,1)} %all-gather.3.cloned.1.call-done, f32[2048]{0:T(1024)S(1)} %add_divide_fusion), kind=kOutput, calls=%fused_computation.1 | convolution fusion | flops 68744642560 | bytes 100671488 | tf_op jit(solution)/shard_map/dot_general | solution.py:19
  (1 shorter events, 0.0 us)
Async XLA Ops:
  6.5 296.1 %all-gather.5.cloned.1.call-start = ((), (), s32[]{:S(2)}) async-start(), calls=%async_computation.2 | async-start | bytes 20971520 | tf_op jit(solution)/shard_map/all_gather | solution.py:14
  13.0 590.5 %all-gather.3.cloned.1.call-start = ((), (), s32[]{:S(2)}) async-start(), calls=%async_computation.1 | async-start | bytes 20971520 | tf_op jit(solution)/shard_map/all_gather | solution.py:17
  302.6 8.6 %copy-start = (f32[2048]{0:T(1024)S(1)}, f32[2048]{0:T(1024)}, u32[]{:S(2)}) copy-start(f32[2048]{0:T(1024)} %param.6) | copy-start | bytes 24580
  302.6 280.2 %all-to-all-start = ((bf16[512,4,4096]{0,2,1:T(8,128)(2,1)}), bf16[512,4,4096]{0,2,1:T(8,128)(2,1)}, u32[]{:S(2)}, u32[]{:S(2)}) async-start(bf16[512,4,4096]{0,2,1:T(8,128)(2,1)} %bitcast.8), calls=%async_computation | async-start | bytes 33554432 | tf_op jit(solution)/shard_map/all_to_all | solution.py:15
Sparse Core Ops, SparseCore 0:
  13.1 289.4 all-gather.4
  304.2 194.0 all-gather.2
where the time goes:
time: 692 us; the launch traced here: 691 us
  waiting for transfers between devices  561 us (81%)
  matrix products  81.2 us (12%)
  local copies, waits for them, and re-layouts  27.1 us (4%)
  between operations  14.7 us (2%)
  starting transfers between devices  7.3 us (1%)
    all_gather x1, waiting for transfers between devices, shards(): row_full = lax.all_gather(pair_block, 'col', axis=1, tiled=True)  289 us
    all_to_all x1, waiting for transfers between devices, shards(): lax.all_to_all(row_full, 'blk', split_axis=1, concat_axis=0, tiled=True)  272 us
    dot_general x1, matrix products, shards(): lax.dot_general(scaled, column_slab, (((0,), (0,)), ((), ())), preferred_...  81.2 us
    all_to_all x1, local copies, waits for them, and re-layouts, shards(): lax.all_to_all(row_full, 'blk', split_axis=1, concat_axis=0, tiled=True)  20.7 us
  transfers between devices with their start and end apart: 3, of which 2 were waited for; matrix products, arithmetic and copies ran while one was open for 3% of the time, Pallas kernels for 0%

commit v1 on v0

--- a/solution.py
+++ b/solution.py
@@ -10,8 +10,21 @@
 
 
 def shards(pair_block, occ_energy, virt_energy, frequency):
+
+    def run_words_for(u, ax_name, dim_k):
+        width = lax.axis_size(ax_name)
+        newest = sorted(((b, (b + 1) % width) for b in range(width)))
+        g_now = u
+        items = [g_now]
+        for dd in range(1, width):
+            g_now = lax.ppermute(g_now, ax_name, newest)
+            items.insert(0, g_now)
+        taken_in = jnp.concatenate(items, axis=dim_k)
+        value_now = lax.axis_index(ax_name)
+        return jnp.roll(taken_in, shift=(value_now + 1) * u.shape[dim_k], axis=dim_k)
+
     weights = pair_weights(occ_energy, virt_energy, frequency)
-    row_full = lax.all_gather(pair_block, "col", axis=1, tiled=True)
+    row_full = run_words_for(pair_block, "col", dim_k=1)
     column_slab = lax.all_to_all(row_full, "blk", split_axis=1, concat_axis=0, tiled=True)
     scaled = (
         lax.all_gather(pair_block, "blk", axis=0, tiled=True).astype(jnp.float32) * weights[:, None]

time: 692 us -> 644 us (0.931)
  waiting for transfers between devices: 561 us -> 461 us
  local copies, waits for them, and re-layouts: 27.1 us -> 75.3 us
    all_gather x1 -> x0, waiting for transfers between devices: 289 us -> none  [shards(): row_full = lax.all_gather(pair_block, 'col', axis=1, tiled=True)]
    ppermute x0 -> x3, waiting for transfers between devices: none -> 280 us  [run_words_for(): g_now = lax.ppermute(g_now, ax_name, newest)]
    all_to_all x1, waiting for transfers between devices: 272 us -> 182 us  [shards(): lax.all_to_all(row_full, 'blk', split_axis=1, concat_axis=0, tiled=True)]
    unnamed x3 -> x12, local copies, waits for them, and re-layouts: 6.4 us -> 37.8 us
    dynamic_slice x0 -> x1, local copies, waits for them, and re-layouts: none -> 13.7 us  [run_words_for(): jnp.roll(taken_in, shift=(value_now + 1) * u.shape[dim_k], axis=dim_k)]
  transfers between devices with their start and end apart: 3 -> 5, of which waited for: 2 -> 4; matrix products, arithmetic and copies ran while one was open for 3% -> 11% of each run, Pallas kernels for 0% -> 0%
where the time goes in v1:
time: 644 us; the launch traced here: 643 us
  waiting for transfers between devices  461 us (72%)
  matrix products  81.1 us (13%)
  local copies, waits for them, and re-layouts  75.3 us (12%)
  between operations  14.7 us (2%)
  starting transfers between devices  10.2 us (2%)
    ppermute x3, waiting for transfers between devices, run_words_for(): g_now = lax.ppermute(g_now, ax_name, newest)  280 us
    all_to_all x1, waiting for transfers between devices, shards(): lax.all_to_all(row_full, 'blk', split_axis=1, concat_axis=0, tiled=True)  182 us
    dot_general x1, matrix products, shards(): lax.dot_general(scaled, column_slab, (((0,), (0,)), ((), ())), preferred_...  81.1 us
    unnamed x12, local copies, waits for them, and re-layouts  37.8 us
    all_to_all x1, local copies, waits for them, and re-layouts, shards(): lax.all_to_all(row_full, 'blk', split_axis=1, concat_axis=0, tiled=True)  21.5 us
    dynamic_slice x1, local copies, waits for them, and re-layouts, run_words_for(): jnp.roll(taken_in, shift=(value_now + 1) * u.shape[dim_k], axis=dim_k)  13.7 us
  transfers between devices with their start and end apart: 5, of which 4 were waited for; matrix products, arithmetic and copies ran while one was open for 11% of the time, Pallas kernels for 0%

profile of v1, /device:TPU:0, one launch (start us, length us, event | category | flops | bytes accessed | tf_op | source)
XLA Modules:
  0.0 642.6 jit_solution(11457344198630002938)
XLA Ops:
  6.5 0.0 all-gather.2.cloned.1.call-start
  6.5 6.5 %copy.5 = bf16[512,4096]{0,1:T(8,128)(2,1)} copy(bf16[512,4096]{1,0:T(8,128)(2,1)} %param.4) | data formatting | bytes 8388608 | tf_op args[0]
  13.0 3.1 collective-permute-start
  16.1 92.9 %collective-permute-done = bf16[512,4096]{0,1:T(8,128)(2,1)} collective-permute-done((bf16[512,4096]{0,1:T(8,128)(2,1)}, bf16[512,4096]{0,1:T(8,128)(2,1)}, u32[]{:S(2)}, u32[]{:S(2)}) %collective-permute-start) | collective-permute-done | bytes 4194336 | tf_op jit(solution)/shard_map/ppermute | solution.py:20
  109.0 0.0 collective-permute-start.1
  109.0 0.0 all-gather.2.cloned.1.call-update
  109.0 93.8 %collective-permute-done.1 = bf16[512,4096]{0,1:T(8,128)(2,1)} collective-permute-done((bf16[512,4096]{0,1:T(8,128)(2,1)}, bf16[512,4096]{0,1:T(8,128)(2,1)}, u32[]{:S(2)}, u32[]{:S(2)}) %collective-permute-start.1) | collective-permute-done | bytes 4194336 | tf_op jit(solution)/shard_map/ppermute | solution.py:20
  202.8 0.0 collective-permute-start.2
  202.8 0.0 copy-start
  202.8 93.0 %collective-permute-done.2 = bf16[512,4096]{0,1:T(8,128)(2,1)} collective-permute-done((bf16[512,4096]{0,1:T(8,128)(2,1)}, bf16[512,4096]{0,1:T(8,128)(2,1)}, u32[]{:S(2)}, u32[]{:S(2)}) %collective-permute-start.2) | collective-permute-done | bytes 4194336 | tf_op jit(solution)/shard_map/ppermute | solution.py:20
  295.8 4.5 constant_dynamic-update-slice_fusion.7
  300.3 4.5 constant_dynamic-update-slice_fusion.6
  304.8 4.5 constant_dynamic-update-slice_fusion.5
  309.2 4.5 constant_dynamic-update-slice_fusion.4
  313.7 4.5 constant_dynamic-update-slice_fusion.3
  318.2 4.5 constant_dynamic-update-slice_fusion.2
  322.6 4.5 constant_dynamic-update-slice_fusion.1
  327.1 0.0 copy-done
  327.1 2.3 constant_dynamic-update-slice_fusion
  329.4 0.0 copy-start.1
  329.4 13.7 %constant_dynamic-slice_fusion = bf16[512,16384]{0,1:T(8,128)(2,1)} fusion(bf16[512,32768]{0,1:T(8,128)(2,1)} %constant_dynamic-update-slice_fusion, s32[]{:T(128)S(6)} %select_n.14), kind=kLoop, calls=%fused_computation.12 | loop fusion | bytes 33554436 | tf_op jit(solution)/shard_map/jit(_roll_dynamic)/dynamic_slice | solution.py:24
  343.1 7.2 %all-to-all-start = ((bf16[512,4,4096]{0,2,1:T(8,128)(2,1)}), bf16[512,4,4096]{0,2,1:T(8,128)(2,1)}, u32[]{:S(2)}, u32[]{:S(2)}) async-start(bf16[512,4,4096]{0,2,1:T(8,128)(2,1)} %bitcast.8), calls=%async_computation | async-start | bytes 33554432 | tf_op jit(solution)/shard_map/all_to_all | solution.py:28
  351.6 0.0 copy-done.1
  351.6 181.5 %all-to-all-done = bf16[512,4,4096]{0,2,1:T(8,128)(2,1)} async-done(((bf16[512,4,4096]{0,2,1:T(8,128)(2,1)}), bf16[512,4,4096]{0,2,1:T(8,128)(2,1)}, u32[]{:S(2)}, u32[]{:S(2)}) %all-to-all-start) | async-done | bytes 16777248 | tf_op jit(solution)/shard_map/all_to_all | solution.py:28
  533.1 21.5 %copy.8 = bf16[4,512,4096]{2,1,0:T(8,128)(2,1)} copy(bf16[4,512,4096]{1,2,0:T(8,128)(2,1)} %bitcast.3) | data formatting | bytes 33554432 | tf_op jit(solution)/shard_map/all_to_all | solution.py:28
  554.6 0.0 all-gather.2.cloned.1.call-done
  554.6 81.1 %fusion = f32[4096,4096]{1,0:T(8,128)} fusion(bf16[2048,4096]{1,0:T(8,128)(2,1)} %bitcast.9, bf16[2048,4096]{1,0:T(8,128)(2,1)} %all-gather.2.cloned.1.call-done, f32[2048]{0:T(1024)S(1)} %add_divide_fusion), kind=kOutput, calls=%fused_computation.1 | convolution fusion | flops 68744642560 | bytes 100671488 | tf_op jit(solution)/shard_map/dot_general | solution.py:32
  (1 shorter events, 0.0 us)
Async XLA Ops:
  6.5 548.1 %all-gather.2.cloned.1.call-start = ((), (), s32[]{:S(2)}) async-start(), calls=%async_computation.1 | async-start | bytes 20971520 | tf_op jit(solution)/shard_map/all_gather | solution.py:30
  13.0 96.0 %collective-permute-start = (bf16[512,4096]{0,1:T(8,128)(2,1)}, bf16[512,4096]{0,1:T(8,128)(2,1)}, u32[]{:S(2)}, u32[]{:S(2)}) collective-permute-start(bf16[512,4096]{0,1:T(8,128)(2,1)} %copy.5), channel_id=1, source_target_pairs={{0,1},{1,2},{2,3},{3,0},{4,5},{5,6},{6,7},{7,4},{8,9},{9,10},{10,1... | collective-permute-start | bytes 12582920 | tf_op jit(solution)/shard_map/ppermute | solution.py:20
  109.0 93.8 %collective-permute-start.1 = (bf16[512,4096]{0,1:T(8,128)(2,1)}, bf16[512,4096]{0,1:T(8,128)(2,1)}, u32[]{:S(2)}, u32[]{:S(2)}) collective-permute-start(bf16[512,4096]{0,1:T(8,128)(2,1)} %collective-permute-done), channel_id=1, source_target_pairs={{0,1},{1,2},{2,3},{3,0},{4,5},{5,6},{6,7},{7,4},{8,9},{9,10},{10,1... | collective-permute-start | bytes 12582920 | tf_op jit(solution)/shard_map/ppermute | solution.py:20
  202.8 93.0 %collective-permute-start.2 = (bf16[512,4096]{0,1:T(8,128)(2,1)}, bf16[512,4096]{0,1:T(8,128)(2,1)}, u32[]{:S(2)}, u32[]{:S(2)}) collective-permute-start(bf16[512,4096]{0,1:T(8,128)(2,1)} %collective-permute-done.1), channel_id=1, source_target_pairs={{0,1},{1,2},{2,3},{3,0},{4,5},{5,6},{6,7},{7,4},{8,9},{9,10},{10,1... | collective-permute-start | bytes 12582920 | tf_op jit(solution)/shard_map/ppermute | solution.py:20
  202.8 124.3 %copy-start = (bf16[512,4096]{0,1:T(8,128)(2,1)S(1)}, bf16[512,4096]{0,1:T(8,128)(2,1)}, u32[]{:S(2)}) copy-start(bf16[512,4096]{0,1:T(8,128)(2,1)} %copy.5) | copy-start | bytes 12582916
  329.4 22.2 %copy-start.1 = (f32[2048]{0:T(1024)S(1)}, f32[2048]{0:T(1024)}, u32[]{:S(2)}) copy-start(f32[2048]{0:T(1024)} %param.6) | copy-start | bytes 24580
  343.1 190.0 %all-to-all-start = ((bf16[512,4,4096]{0,2,1:T(8,128)(2,1)}), bf16[512,4,4096]{0,2,1:T(8,128)(2,1)}, u32[]{:S(2)}, u32[]{:S(2)}) async-start(bf16[512,4,4096]{0,2,1:T(8,128)(2,1)} %bitcast.8), calls=%async_computation | async-start | bytes 33554432 | tf_op jit(solution)/shard_map/all_to_all | solution.py:28
Sparse Core Ops, SparseCore 0:
  109.1 107.3 all-gather.1
